TPU v7x, 32 devices: a whole 2x2x4 slice. The times are simulated.
32 devices in a mesh: seq: 8 (over z, core), batch: 4 (over y, x).
Axes of the slice: x: 2, y: 2, z: 4, core: 2. Of those that a mesh axis runs over, the one named last changes fastest.
Arguments:
- tokens: bfloat16 [4, 2048, 1152], P('batch', 'seq'), may hold values from -6 to 6
- long_skip: bfloat16 [4, 2048, 1152], P('batch', 'seq'), may hold values from -6 to 6
- lengths: int32 [4, 4], P('batch'), may hold values from 0 to 1026, as said below
- skip_weight: bfloat16 [2304, 1152], replicated, may hold values from -0.125 to 0.125
- skip_bias: bfloat16 [1152], replicated, may hold values from -3 to 3
- attention_gain: bfloat16 [1152], replicated, may hold values from 0.099609375 to 1.8984375
- attention_shift: bfloat16 [1152], replicated, may hold values from -3 to 3
- qkv_weight: bfloat16 [1152, 3456], replicated, may hold values from -0.1875 to 0.1875
- out_weight: bfloat16 [1152, 1152], replicated, may hold values from -2 to 2
- out_bias: bfloat16 [1152], replicated, may hold values from -3 to 3
- mlp_gain: bfloat16 [1152], replicated, may hold values from 0.099609375 to 1.8984375
- mlp_shift: bfloat16 [1152], replicated, may hold values from -3 to 3
- hidden_weight: bfloat16 [1152, 4608], replicated, may hold values from -0.1875 to 0.1875
- hidden_bias: bfloat16 [4608], replicated, may hold values from -3 to 3
- down_weight: bfloat16 [4608, 1152], replicated, may hold values from -0.09375 to 0.09375
- down_bias: bfloat16 [1152], replicated, may hold values from -3 to 3
- cotangent: bfloat16 [4, 2048, 1152], P('batch', 'seq'), may hold values from -6 to 6
Outputs:
- output: bfloat16 [4, 2048, 1152], P('batch', 'seq')
- grad_tokens: float32 [4, 2048, 1152], P('batch', 'seq')
- grad_long_skip: float32 [4, 2048, 1152], P('batch', 'seq')
- grad_skip_weight: float32 [2304, 1152], P('batch', 'seq')
- grad_skip_bias: float32 [1152], replicated
- grad_attention_gain: float32 [1152], replicated
- grad_attention_shift: float32 [1152], replicated
- grad_qkv_weight: float32 [1152, 3456], P('batch', 'seq')
- grad_out_weight: float32 [1152, 1152], P('batch', 'seq')
- grad_out_bias: float32 [1152], replicated
- grad_mlp_gain: float32 [1152], replicated
- grad_mlp_shift: float32 [1152], replicated
- grad_hidden_weight: float32 [1152, 4608], P('batch', 'seq')
- grad_hidden_bias: float32 [4608], replicated
- grad_down_weight: float32 [4608, 1152], P('batch', 'seq')
- grad_down_bias: float32 [1152], replicated
Inputs may be any that keep to these rules, and one draw needn't show every extreme that they name: Row g lists the lengths of group g's items in the order in which they lie along the group's 2048 positions. Each entry is 258, 1026 or 0, every row has one or more entries 1026, zeros stand only after the last nonzero entry, and the row's total leaves fewer than 258 positions of padding at the end.
All inputs are finite; a program needn't handle non-finite values.
Results may differ from a plain program's by a relative error of at most 0.013.
Values may be sent and summed in bfloat16 or wider, within the bound.
A program may use at most 256 MiB of HBM per device.

v0:
```python
import math
import jax
import jax.numpy as jnp
from jax import lax
from jax.sharding import PartitionSpec as P

HD = 72
norm_eps = 1e-05


def product(left, right):
    return jnp.dot(left, right, preferred_element_type=jnp.float32)


def contract_rows(left, right):
    return lax.dot_general(
        left, right, (((0,), (0,)), ((), ())), preferred_element_type=jnp.float32
    )


def times_transposed(left, right):
    return lax.dot_general(
        left, right, (((1,), (1,)), ((), ())), preferred_element_type=jnp.float32
    )


def column_sums(values):
    return jnp.sum(values.astype(jnp.float32), axis=0)


def layer_norm(inputs, gain, shift):
    mean_row = jnp.mean(inputs, axis=-1, keepdims=True)
    centred = inputs - mean_row
    spread = jnp.mean(centred * centred, axis=-1, keepdims=True)
    return centred * lax.rsqrt(spread + norm_eps) * gain + shift


def exact_gelu(inputs):
    return jax.nn.gelu(inputs, approximate=False)


def segments(row_lengths, group_len):
    ends = jnp.cumsum(row_lengths)
    places = jnp.arange(group_len, dtype=jnp.int32)
    return jnp.sum((places[:, None] >= ends[None, :]).astype(jnp.int32), axis=1)


def score_block(query_block, key_heads, seg_block, segment):
    raw = jnp.einsum("bhd,khd->hbk", query_block, key_heads, preferred_element_type=jnp.float32)
    scores = raw * (1.0 / math.sqrt(HD))
    allowed = (seg_block[:, None] == segment[None, :])[None]
    return jnp.where(allowed, scores, -jnp.inf)


def attend_forward(query_heads, key_flat, value_flat, segment):
    length, head_cols = query_heads.shape
    head_count = head_cols // HD
    block_rows = min(512, length)
    block_count = length // block_rows
    key_heads = key_flat.reshape(length, head_count, HD)
    value_heads = value_flat.reshape(length, head_count, HD)

    def one_block(pieces):
        query_block, seg_block = pieces
        scores = score_block(query_block, key_heads, seg_block, segment)
        row_max = jnp.max(scores, axis=2, keepdims=True)
        log_total = row_max + jnp.log(jnp.sum(jnp.exp(scores - row_max), axis=2, keepdims=True))
        probs_low = jnp.exp(scores - log_total).astype(jnp.bfloat16)
        context = jnp.einsum(
            "hbk,khd->bhd", probs_low, value_heads, preferred_element_type=jnp.float32
        )
        return (context.astype(jnp.bfloat16).reshape(block_rows, head_cols), log_total)

    context, log_total = lax.map(
        one_block,
        (
            query_heads.reshape(block_count, block_rows, head_count, HD),
            segment.reshape(block_count, block_rows),
        ),
    )
    return (context.reshape(length, head_cols), log_total)


def attend_backward(query_heads, key_flat, value_flat, segment, grad_context, log_total):
    length, head_cols = query_heads.shape
    head_count = head_cols // HD
    block_rows = min(512, length)
    block_count = length // block_rows
    score_scale = 1.0 / math.sqrt(HD)
    key_heads = key_flat.reshape(length, head_count, HD)
    value_heads = value_flat.reshape(length, head_count, HD)

    def one_block(totals, pieces):
        grad_keys, grad_values = totals
        query_block, seg_block, grad_block, total_block = pieces
        scores = score_block(query_block, key_heads, seg_block, segment)
        prob_full = jnp.exp(scores - total_block)
        probs_low = prob_full.astype(jnp.bfloat16)
        grad_values = grad_values + jnp.einsum(
            "hbk,bhd->khd", probs_low, grad_block, preferred_element_type=jnp.float32
        )
        grad_probs = jnp.einsum(
            "bhd,khd->hbk", grad_block, value_heads, preferred_element_type=jnp.float32
        )
        row_delta = jnp.sum(prob_full * grad_probs, axis=2, keepdims=True)
        grad_scores = (prob_full * (grad_probs - row_delta)).astype(jnp.bfloat16)
        grad_query = (
            jnp.einsum("hbk,khd->bhd", grad_scores, key_heads, preferred_element_type=jnp.float32)
            * score_scale
        )
        grad_keys = grad_keys + jnp.einsum(
            "hbk,bhd->khd", grad_scores, query_block, preferred_element_type=jnp.float32
        )
        return (
            (grad_keys, grad_values),
            grad_query.astype(jnp.bfloat16).reshape(block_rows, head_cols),
        )

    empty_sum = jnp.zeros((length, head_count, HD), jnp.float32)
    (grad_keys, grad_values), grad_query = lax.scan(
        one_block,
        (empty_sum, empty_sum),
        (
            query_heads.reshape(block_count, block_rows, head_count, HD),
            segment.reshape(block_count, block_rows),
            grad_context.reshape(block_count, block_rows, head_count, HD),
            log_total,
        ),
    )
    grad_keys = (grad_keys * score_scale).astype(jnp.bfloat16).reshape(length, head_cols)
    grad_values = grad_values.astype(jnp.bfloat16).reshape(length, head_cols)
    return (grad_query.reshape(length, head_cols), grad_keys, grad_values)


def seq_gathered_grad(left, right):
    left_all = lax.all_gather(left, "seq", axis=0, tiled=True)
    right_cols = lax.all_to_all(right, "seq", split_axis=1, concat_axis=0, tiled=True)
    partial = contract_rows(left_all, right_cols).astype(jnp.bfloat16)
    summed = lax.psum_scatter(partial, "batch", scatter_dimension=0, tiled=True)
    return summed.astype(jnp.float32)


def batch_gathered_grad(left, right):
    left_rows = lax.all_to_all(left, "batch", split_axis=1, concat_axis=0, tiled=True)
    right_all = lax.all_gather(right, "batch", axis=0, tiled=True)
    partial = contract_rows(left_rows, right_all).astype(jnp.bfloat16)
    summed = lax.psum_scatter(partial, "seq", scatter_dimension=1, tiled=True)
    return summed.astype(jnp.float32)


def qkv_grad_from_heads(left, grad_heads):
    seq_count = lax.axis_size("seq")
    me = lax.axis_index("seq")
    piece = grad_heads.shape[1] // 3
    left_all = lax.all_gather(left, "seq", axis=0, tiled=True)
    partial = contract_rows(left_all, grad_heads).astype(jnp.bfloat16)
    summed = lax.psum_scatter(partial, "batch", scatter_dimension=0, tiled=True)
    summed = summed.astype(jnp.float32)
    inverse = pow(3, -1, seq_count)
    slots = []
    for slot in range(3):
        target = (me - slot) * inverse % seq_count
        chunk = (3 * target + slot) // seq_count
        sent = lax.dynamic_slice_in_dim(summed, chunk * piece, piece, axis=1)
        pairs = []
        for source in range(seq_count):
            pairs.append((source, (source - slot) * inverse % seq_count))
        slots.append(lax.ppermute(sent, "seq", pairs))
    return jnp.concatenate(slots, axis=1)


GRAD_PLAN = {"skip": "batch", "qkv": "seq", "out": "batch", "hidden": "seq", "down": "batch"}


def weight_grad(name, left, right):
    if GRAD_PLAN[name] == "seq":
        return seq_gathered_grad(left, right)
    return batch_gathered_grad(left, right)


def on_device(
    tokens,
    long_skip,
    lengths,
    skip_weight,
    skip_bias,
    attention_gain,
    attention_shift,
    qkv_weight,
    out_weight,
    out_bias,
    mlp_gain,
    mlp_shift,
    hidden_weight,
    hidden_bias,
    down_weight,
    down_bias,
    cotangent,
):
    local_rows = tokens.shape[1]
    feature_count = tokens.shape[2]
    group_len = local_rows * lax.axis_size("seq")
    joined = jnp.concatenate([tokens[0], long_skip[0]], axis=1)
    mixed = product(joined, skip_weight) + skip_bias.astype(jnp.float32)
    normed_full, first_pull = jax.vjp(
        layer_norm, mixed, attention_gain.astype(jnp.float32), attention_shift.astype(jnp.float32)
    )
    normed_one = normed_full.astype(jnp.bfloat16)
    packed = product(normed_one, qkv_weight).astype(jnp.bfloat16)
    seq_count = lax.axis_size("seq")
    packed_heads = lax.all_to_all(
        packed.reshape(local_rows, 3, seq_count, feature_count // seq_count),
        "seq",
        split_axis=2,
        concat_axis=0,
        tiled=True,
    ).reshape(group_len, 3, feature_count // seq_count)
    query_heads = packed_heads[:, 0]
    key_heads = packed_heads[:, 1]
    value_heads = packed_heads[:, 2]
    segment = segments(lengths[0], group_len)
    context_heads, log_total = attend_forward(query_heads, key_heads, value_heads, segment)
    context_tok = lax.all_to_all(context_heads, "seq", split_axis=0, concat_axis=1, tiled=True)
    middle = mixed + product(context_tok, out_weight) + out_bias.astype(jnp.float32)
    second_full, second_pull = jax.vjp(
        layer_norm, middle, mlp_gain.astype(jnp.float32), mlp_shift.astype(jnp.float32)
    )
    normed_two = second_full.astype(jnp.bfloat16)
    hidden_pre = product(normed_two, hidden_weight) + hidden_bias.astype(jnp.float32)
    act_full, gelu_pull = jax.vjp(exact_gelu, hidden_pre)
    hidden_act = act_full.astype(jnp.bfloat16)
    output = (middle + product(hidden_act, down_weight) + down_bias.astype(jnp.float32)).astype(
        jnp.bfloat16
    )
    grad_out_rows = cotangent[0]
    grad_down_weight = weight_grad("down", hidden_act, grad_out_rows)
    grad_down_bias = column_sums(grad_out_rows)
    grad_act = times_transposed(grad_out_rows, down_weight)
    grad_pre = gelu_pull(grad_act)[0].astype(jnp.bfloat16)
    grad_hidden_weight = weight_grad("hidden", normed_two, grad_pre)
    grad_hidden_bias = column_sums(grad_pre)
    grad_normed_two = times_transposed(grad_pre, hidden_weight)
    grad_middle_norm, grad_mlp_gain, grad_mlp_shift = second_pull(grad_normed_two)
    grad_middle = grad_out_rows.astype(jnp.float32) + grad_middle_norm
    grad_attended = grad_middle.astype(jnp.bfloat16)
    grad_out_bias = column_sums(grad_attended)
    grad_out_weight = weight_grad("out", context_tok, grad_attended)
    grad_context = times_transposed(grad_attended, out_weight).astype(jnp.bfloat16)
    grad_context_heads = lax.all_to_all(
        grad_context, "seq", split_axis=1, concat_axis=0, tiled=True
    )
    grad_query, grad_key, grad_value = attend_backward(
        query_heads, key_heads, value_heads, segment, grad_context_heads, log_total
    )
    grad_packed = jnp.concatenate(
        [
            lax.all_to_all(grad_query, "seq", split_axis=0, concat_axis=1, tiled=True),
            lax.all_to_all(grad_key, "seq", split_axis=0, concat_axis=1, tiled=True),
            lax.all_to_all(grad_value, "seq", split_axis=0, concat_axis=1, tiled=True),
        ],
        axis=1,
    )
    grad_qkv_weight = qkv_grad_from_heads(
        normed_one, jnp.concatenate([grad_query, grad_key, grad_value], axis=1)
    )
    grad_normed_one = times_transposed(grad_packed, qkv_weight)
    grad_mixed_norm, grad_attention_gain, grad_attention_shift = first_pull(grad_normed_one)
    grad_mixed = (grad_middle + grad_mixed_norm).astype(jnp.bfloat16)
    grad_skip_bias = column_sums(grad_mixed)
    grad_skip_weight = weight_grad("skip", joined, grad_mixed)
    grad_joined = times_transposed(grad_mixed, skip_weight)
    grad_tokens = grad_joined[:, :feature_count][None]
    grad_long_skip = grad_joined[:, feature_count:][None]
    summed_weights = (
        grad_skip_weight,
        grad_qkv_weight,
        grad_out_weight,
        grad_hidden_weight,
        grad_down_weight,
    )
    small_grads = (
        grad_skip_bias,
        grad_attention_gain,
        grad_attention_shift,
        grad_out_bias,
        grad_mlp_gain,
        grad_mlp_shift,
        grad_hidden_bias,
        grad_down_bias,
    )
    small_sizes = [piece.shape[0] for piece in small_grads]
    small_total = lax.psum(jnp.concatenate(small_grads), ("seq", "batch"))
    summed_small = []
    offset = 0
    for size in small_sizes:
        summed_small.append(small_total[offset : offset + size])
        offset += size
    return (
        output[None],
        grad_tokens,
        grad_long_skip,
        summed_weights[0],
        summed_small[0],
        summed_small[1],
        summed_small[2],
        summed_weights[1],
        summed_weights[2],
        summed_small[3],
        summed_small[4],
        summed_small[5],
        summed_weights[3],
        summed_small[6],
        summed_weights[4],
        summed_small[7],
    )


def solution(mesh):
    in_specs = (
        P("batch", "seq", None),
        P("batch", "seq", None),
        P("batch", None),
        P(),
        P(),
        P(),
        P(),
        P(),
        P(),
        P(),
        P(),
        P(),
        P(),
        P(),
        P(),
        P(),
        P("batch", "seq", None),
    )
    out_specs = (
        P("batch", "seq", None),
        P("batch", "seq", None),
        P("batch", "seq", None),
        P("batch", "seq"),
        P(),
        P(),
        P(),
        P("batch", "seq"),
        P("batch", "seq"),
        P(),
        P(),
        P(),
        P("batch", "seq"),
        P(),
        P("batch", "seq"),
        P(),
    )
    return jax.shard_map(
        on_device, mesh=mesh, in_specs=in_specs, out_specs=out_specs, check_vma=False
    )
```

profile of v0, /device:TPU:0, one launch (start us, length us, event | category | flops | bytes accessed | tf_op | source)
XLA Modules:
  0.0 722.0 jit_solution(6150779179004533748)
XLA Ops:
  9.4 4.7 fusion.79
  16.0 7.2 %convolution_convert_fusion.1 = bf16[256,3456]{1,0:T(8,128)(2,1)} fusion(bf16[256,1152]{1,0:T(8,128)(2,1)S(1)} %add_convert_fusion.3, bf16[1152,3456]{1,0:T(8,128)(2,1)} %param.28), kind=kOutput, calls=%fused_computation.53 | convolution fusion | flops 2039316480 | bytes 10321920 | tf_op jit(solution)/shard_map/dot_general | solution.py:12
  29.9 6.6 all-to-all-start
  36.8 41.7 %all-to-all-done = bf16[256,3,8,144]{0,3,1,2:T(8,128)(2,1)} async-done(((bf16[256,3,8,144]{0,3,1,2:T(8,128)(2,1)}), bf16[256,3,8,144]{0,3,1,2:T(8,128)(2,1)}, u32[]{:S(2)}, u32[]{:S(2)}) %all-to-all-start) | async-done | bytes 1769504 | tf_op jit(solution)/shard_map/all_to_all | solution.py:211
  93.8 36.5 %while.27 = (s32[]{:T(128)}, bf16[4,512,144]{1,2,0:T(8,128)(2,1)}, f32[4,2,512,1]{2,1,3,0:T(2,128)S(1)}, s32[4,512]{1,0:T(4,128)S(1)}, s32[2048]{0:T(1024)S(1)},...) while((s32[]{:T(128)}, bf16[4,512,144]{1,2,0:T(8,128)(2,1)}, ...), condition=%wide.region_7.8_spmd, body=%wide.region_4.7_spmd.sunk | while | flops 628169728 | bytes 33536144 | solution.py:74
  137.0 4.2 all-to-all-start.1
  142.0 20.8 %all-to-all-done.1 = bf16[8,256,144]{1,2,0:T(8,128)(2,1)} async-done(((bf16[8,256,144]{1,2,0:T(8,128)(2,1)}), bf16[8,256,144]{1,2,0:T(8,128)(2,1)}, u32[]{:S(2)}, u32[]{:S(2)}) %all-to-all-start.1) | async-done | bytes 589856 | tf_op jit(solution)/shard_map/all_to_all | solution.py:223
  167.6 17.2 %multiply_convert_fusion.1 = (bf16[256,4608]{1,0:T(8,128)(2,1)}, f32[256,4608]{1,0:T(8,128)}, f32[256,4608]{1,0:T(8,128)}) fusion(f32[4608]{0:T(1024)S(1)} %convert_element_type.134, bf16[256,1152]{1,0:T(8,128)(2,1)} %add_convert_fusion.2, bf16[1152,4608]{1,0:T(8,128)(2,1)} %param.33), kind=kOutput, calls=%fused_computation.57 | convolution fusion | flops 2795765760 | bytes 23021568 | tf_op jit(solution)/shard_map/dot_general | solution.py:12
  184.8 14.7 %convert_reduce_fusion = (f32[4608]{0:T(1024)}, bf16[256,4608]{1,0:T(8,128)(2,1)}) fusion(f32[256,4608]{1,0:T(8,128)} %get-tuple-element.290, f32[256,4608]{1,0:T(8,128)} %get-tuple-element.315, bf16[4608,1152]{1,0:T(8,128)(2,1)} %param.35, bf16[1,256,1152]{2,1,0:T(8,128)(2,1)S(1)} %copy-done.14), kind=kOutput, calls=%fused_computation.55 | convolution fusion | flops 2736778752 | bytes 23021568 | tf_op jit(solution)/shard_map/dot_general | solution.py:22
  199.5 8.7 %multiply_reduce_fusion.1 = (f32[1152]{0:T(1024)}, f32[256]{0:T(256)S(1)}, f32[1152]{0:T(1024)}, f32[256,1152]{1,0:T(8,128)S(1)}) fusion(f32[256,1152]{1,0:T(8,128)S(1)} %copy-done.7, f32[256]{0:T(256)S(1)} %fusion.69, f32[256]{0:T(256)S(1)} %broadcast_multiply_fusion, f32[1152]{0:T(1024)S(1)} %convert_element_type.131, ...), kind=kOutput, calls=%fused_computation.106 | convolution fusion | flops 2720265728 | bytes 15352320 | tf_op jit(solution)/shard_map/dot_general | solution.py:22
  220.7 15.9 %all-to-all-done.2 = bf16[256,8,144]{0,2,1:T(8,128)(2,1)S(1)} async-done(((bf16[256,8,144]{0,2,1:T(8,128)(2,1)}), bf16[256,8,144]{0,2,1:T(8,128)(2,1)S(1)}, u32[]{:S(2)}, u32[]{:S(2)}) %all-to-all-start.2) | async-done | bytes 589856 | tf_op jit(solution)/shard_map/all_to_all | solution.py:249
  239.0 87.2 %while.28 = (s32[]{:T(128)}, f32[2048,2,72]{0,2,1:T(8,128)S(1)}, f32[2048,2,72]{0,2,1:T(8,128)}, bf16[4,512,144]{1,2,0:T(8,128)(2,1)}, bf16[4,512,2,72]{1,3,2,0:...) while((s32[]{:T(128)}, f32[2048,2,72]{0,2,1:T(8,128)S(1)}, ...), condition=%wide.region_14.15_spmd.clone, body=%wide.region_12.14_spmd.clone.sunk | while | flops 1543781376 | bytes 136800560 | solution.py:120
  242.0 4.3 multiply_reduce_fusion.8
  246.2 3.9 multiply_convert_fusion.4
  253.5 5.1 fusion.146
  263.8 4.3 multiply_reduce_fusion.8
  268.0 3.9 multiply_convert_fusion.4
  275.3 5.2 fusion.146
  285.6 4.3 multiply_reduce_fusion.8
  289.8 3.9 multiply_convert_fusion.4
  297.1 5.2 fusion.146
  307.4 4.3 multiply_reduce_fusion.8
  318.9 5.2 fusion.146
  328.6 4.3 all-to-all-start.5
  334.1 15.5 %all-to-all-done.5 = bf16[8,256,144]{1,2,0:T(8,128)(2,1)} async-done(((bf16[8,256,144]{1,2,0:T(8,128)(2,1)}), bf16[8,256,144]{1,2,0:T(8,128)(2,1)}, u32[]{:S(2)}, u32[]{:S(2)}) %all-to-all-start.5) | async-done | bytes 589856 | tf_op jit(solution)/shard_map/all_to_all | solution.py:259
  349.7 4.2 all-to-all-start.4
  357.3 13.3 %all-to-all-done.4 = bf16[8,256,144]{1,2,0:T(8,128)(2,1)} async-done(((bf16[8,256,144]{1,2,0:T(8,128)(2,1)}), bf16[8,256,144]{1,2,0:T(8,128)(2,1)}, u32[]{:S(2)}, u32[]{:S(2)}) %all-to-all-start.4) | async-done | bytes 589856 | tf_op jit(solution)/shard_map/all_to_all | solution.py:258
  370.6 19.3 %all_to_all.180 = bf16[8,256,144]{1,2,0:T(8,128)(2,1)S(1)} all-to-all(bf16[8,256,144]{1,2,0:T(8,128)(2,1)S(1)} %copy.108), channel_id=1, replica_groups=mesh['seq'=8,'batch'=4] {'seq'}, dimensions={0} | all-to-all | bytes 1179648 | tf_op jit(solution)/shard_map/all_to_all | solution.py:257
  389.9 6.5 multiply_reduce_fusion.2
  399.8 6.0 convolution_convert_fusion.4
  405.9 4.1 all-to-all-start.7
  411.6 9.8 %all-to-all-done.7 = bf16[256,4,288]{0,2,1:T(8,128)(2,1)S(1)} async-done(((bf16[256,4,288]{0,2,1:T(8,128)(2,1)}), bf16[256,4,288]{0,2,1:T(8,128)(2,1)S(1)}, u32[]{:S(2)}, u32[]{:S(2)}) %all-to-all-start.7) | async-done | bytes 589856 | tf_op jit(solution)/shard_map/all_to_all | solution.py:144
  425.9 4.7 convolution_convert_fusion.5
  430.9 34.5 %all-to-all-done.9 = bf16[256,4,1152]{2,0,1:T(8,128)(2,1)S(1)} async-done(((bf16[256,4,1152]{2,0,1:T(8,128)(2,1)}), bf16[256,4,1152]{2,0,1:T(8,128)(2,1)S(1)}, u32[]{:S(2)}, u32[]{:S(2)}) %all-to-all-start.9) | async-done | bytes 2359328 | tf_op jit(solution)/shard_map/all_to_all | solution.py:144
  465.5 6.5 convolution_convert_fusion
  478.0 4.3 copy.116
  482.2 10.3 %all-to-all-done.6 = bf16[256,4,576]{0,2,1:T(8,128)(2,1)S(1)} async-done(((bf16[256,4,576]{0,2,1:T(8,128)(2,1)}), bf16[256,4,576]{0,2,1:T(8,128)(2,1)S(1)}, u32[]{:S(2)}, u32[]{:S(2)}) %all-to-all-start.6) | async-done | bytes 1179680 | tf_op jit(solution)/shard_map/all_to_all | solution.py:144
  493.5 4.5 all-to-all-start.8
  500.5 5.2 convolution_convert_fusion.3
  506.3 61.5 %all-to-all-done.8 = bf16[256,8,576]{0,2,1:T(8,128)(2,1)S(1)} async-done(((bf16[256,8,576]{0,2,1:T(8,128)(2,1)}), bf16[256,8,576]{0,2,1:T(8,128)(2,1)S(1)}, u32[]{:S(2)}, u32[]{:S(2)}) %all-to-all-start.8) | async-done | bytes 2359328 | tf_op jit(solution)/shard_map/all_to_all | solution.py:137
  569.6 8.2 %convolution_convert_fusion.2 = bf16[1152,576]{1,0:T(8,128)(2,1)} fusion(bf16[2048,1152]{1,0:T(8,128)(2,1)} %all-gather.13.cloned.1.call-done, bf16[2048,576]{0,1:T(8,128)(2,1)} %bitcast.219), kind=kOutput, calls=%fused_computation.71 | convolution fusion | flops 2718572544 | bytes 8404992 | tf_op jit(solution)/shard_map/dot_general | solution.py:16
  578.0 8.9 %fusion.47 = bf16[1,256,1152]{2,1,0:T(8,128)(2,1)} fusion(f32[256,1152]{1,0:T(8,128)S(1)} %copy-done.8, bf16[256,4608]{1,0:T(8,128)(2,1)} %get-tuple-element.289, bf16[4608,1152]{1,0:T(8,128)(2,1)} %param.35, f32[1152]{0:T(1024)S(1)} %convert_element_type.136), kind=kOutput, calls=%fused_computation.82 | convolution fusion | flops 2718793728 | bytes 14750208 | tf_op jit(solution)/shard_map/dot_general | solution.py:12
  587.0 38.9 %psum.7 = f32[12672]{0:T(1024)S(1)} all-reduce(f32[12672]{0:T(1024)S(1)} %constant_dynamic-update-slice_fusion), channel_id=1, replica_groups=mesh['seq'=8,'batch'=4] {'seq','batch'}, use_global_device_ids=true, to_apply=%region_26.27 | all-reduce | flops 12672 | bytes 101376 | tf_op jit(solution)/shard_map/psum | solution.py:292
  626.5 4.3 fusion.81
  634.5 4.7 collective-permute-start.2
  642.9 10.9 %collective-permute-done.2 = f32[288,144]{1,0:T(8,128)} collective-permute-done((f32[288,144]{1,0:T(8,128)}, f32[288,144]{1,0:T(8,128)}, u32[]{:S(2)}, u32[]{:S(2)}) %collective-permute-start.2) | collective-permute-done | bytes 165920 | tf_op jit(solution)/shard_map/ppermute | solution.py:168
  657.9 23.6 %reduce-scatter.6.cloned.1.call-done = bf16[576,144]{0,1:T(8,128)(2,1)} async-done(((bf16[576,1152]{0,1:T(8,128)(2,1)}), bf16[576,144]{0,1:T(8,128)(2,1)}) %reduce-scatter.6.cloned.1.call-update) | async-done | bytes 165904 | tf_op jit(solution)/shard_map/reduce_scatter | solution.py:147
  683.2 29.8 %reduce-scatter.12.cloned.1.call-done = bf16[288,576]{1,0:T(8,128)(2,1)} async-done(((bf16[1152,576]{1,0:T(8,128)(2,1)}), bf16[288,576]{1,0:T(8,128)(2,1)}) %reduce-scatter.12.cloned.1.call-update) | async-done | bytes 331792 | tf_op jit(solution)/shard_map/reduce_scatter | solution.py:139
  (304 shorter events, 171.1 us)
Async XLA Ops:
  7.2 155.6 %copy-start = (bf16[1152,1152]{1,0:T(8,128)(2,1)S(1)}, bf16[1152,1152]{1,0:T(8,128)(2,1)}, u32[]{:S(2)}) copy-start(bf16[1152,1152]{1,0:T(8,128)(2,1)} %param.29) | copy-start | bytes 7962628
  16.0 7.2 %copy-start.23 = (bf16[256,1152]{1,0:T(8,128)(2,1)}, bf16[256,1152]{1,0:T(8,128)(2,1)S(1)}, u32[]{:S(2)}) copy-start(bf16[256,1152]{1,0:T(8,128)(2,1)S(1)} %add_convert_fusion.3) | copy-start | bytes 1769476
  27.1 9.4 %copy-start.45 = (s32[1,4]{1,0:T(1,128)S(1)}, s32[1,4]{1,0:T(1,128)}, u32[]{:S(2)}) copy-start(s32[1,4]{1,0:T(1,128)} %param.23) | copy-start | bytes 52
  29.9 48.6 %all-to-all-start = ((bf16[256,3,8,144]{0,3,1,2:T(8,128)(2,1)}), bf16[256,3,8,144]{0,3,1,2:T(8,128)(2,1)}, u32[]{:S(2)}, u32[]{:S(2)}) async-start(bf16[256,3,8,144]{0,3,1,2:T(8,128)(2,1)} %copy.98), calls=%async_computation | async-start | bytes 3538944 | tf_op jit(solution)/shard_map/all_to_all | solution.py:211
  130.3 11.6 %copy-start.41 = (bf16[1152]{0:T(1024)(128)(2,1)S(1)}, bf16[1152]{0:T(1024)(128)(2,1)}, u32[]{:S(2)}) copy-start(bf16[1152]{0:T(1024)(128)(2,1)} %param.30) | copy-start | bytes 6916
  130.3 11.6 %copy-start.34 = (bf16[4608]{0:T(1024)(128)(2,1)S(1)}, bf16[4608]{0:T(1024)(128)(2,1)}, u32[]{:S(2)}) copy-start(bf16[4608]{0:T(1024)(128)(2,1)} %param.34) | copy-start | bytes 27652
  130.3 11.6 %copy-start.42 = (bf16[1152]{0:T(1024)(128)(2,1)S(1)}, bf16[1152]{0:T(1024)(128)(2,1)}, u32[]{:S(2)}) copy-start(bf16[1152]{0:T(1024)(128)(2,1)} %param.32) | copy-start | bytes 6916
  130.4 11.6 %copy-start.43 = (bf16[1152]{0:T(1024)(128)(2,1)S(1)}, bf16[1152]{0:T(1024)(128)(2,1)}, u32[]{:S(2)}) copy-start(bf16[1152]{0:T(1024)(128)(2,1)} %param.31) | copy-start | bytes 6916
  137.0 25.9 %all-to-all-start.1 = ((bf16[8,256,144]{1,2,0:T(8,128)(2,1)}), bf16[8,256,144]{1,2,0:T(8,128)(2,1)}, u32[]{:S(2)}, u32[]{:S(2)}) async-start(bf16[8,256,144]{1,2,0:T(8,128)(2,1)} %copy.102), calls=%async_computation.1 | async-start | bytes 1179648 | tf_op jit(solution)/shard_map/all_to_all | solution.py:223
  141.2 258.6 %all-gather.9.cloned.1.call-start = ((), (), s32[]{:S(2)}) async-start(), calls=%async_computation.17 | async-start | bytes 5308416 | tf_op jit(solution)/shard_map/all_gather | solution.py:155
  167.6 17.2 %copy-start.14 = (bf16[1,256,1152]{2,1,0:T(8,128)(2,1)S(1)}, bf16[1,256,1152]{2,1,0:T(8,128)(2,1)}, u32[]{:S(2)}) copy-start(bf16[1,256,1152]{2,1,0:T(8,128)(2,1)} %param.37) | copy-start | bytes 1769476
  184.8 14.7 %copy-start.7 = (f32[256,1152]{1,0:T(8,128)S(1)}, f32[256,1152]{1,0:T(8,128)}, u32[]{:S(2)}) copy-start(f32[256,1152]{1,0:T(8,128)} %copy-done.6) | copy-start | bytes 3538948
  216.4 20.2 %all-to-all-start.2 = ((bf16[256,8,144]{0,2,1:T(8,128)(2,1)}), bf16[256,8,144]{0,2,1:T(8,128)(2,1)S(1)}, u32[]{:S(2)}, u32[]{:S(2)}) async-start(bf16[256,8,144]{0,2,1:T(8,128)(2,1)} %bitcast.18), calls=%async_computation.2 | async-start | bytes 1179648 | tf_op jit(solution)/shard_map/all_to_all | solution.py:249
  220.0 206.0 %all-gather.11.cloned.1.call-start = ((), (), s32[]{:S(2)}) async-start(), calls=%async_computation.19 | async-start | bytes 2949120 | tf_op jit(solution)/shard_map/all_gather | solution.py:145
  327.5 6.6 copy-start.17
  328.6 26.1 %copy-start.13 = (bf16[4,512,144]{1,2,0:T(8,128)(2,1)S(1)}, bf16[4,512,144]{1,2,0:T(8,128)(2,1)}, u32[]{:S(2)}) copy-start(bf16[4,512,144]{1,2,0:T(8,128)(2,1)} %get-tuple-element.120) | copy-start | bytes 1769476
  328.6 21.1 %all-to-all-start.5 = ((bf16[8,256,144]{1,2,0:T(8,128)(2,1)}), bf16[8,256,144]{1,2,0:T(8,128)(2,1)}, u32[]{:S(2)}, u32[]{:S(2)}) async-start(bf16[8,256,144]{1,2,0:T(8,128)(2,1)} %copy.110), calls=%async_computation.5 | async-start | bytes 1179648 | tf_op jit(solution)/shard_map/all_to_all | solution.py:259
  333.0 24.2 %copy-start.19 = (bf16[2048,2,72]{0,2,1:T(8,128)(2,1)}, bf16[2048,2,72]{0,2,1:T(8,128)(2,1)S(1)}, u32[]{:S(2)}) copy-start(bf16[2048,2,72]{0,2,1:T(8,128)(2,1)S(1)} %multiply_convert_fusion.2) | copy-start | bytes 1769476
  334.1 55.8 %copy-start.10 = (f32[256,1152]{1,0:T(8,128)S(1)}, f32[256,1152]{1,0:T(8,128)}, u32[]{:S(2)}) copy-start(f32[256,1152]{1,0:T(8,128)} %copy-done.9) | copy-start | bytes 3538948
  334.1 55.8 %copy-start.29 = (f32[1152]{0:T(1024)S(1)}, f32[1152]{0:T(1024)}, u32[]{:S(2)}) copy-start(f32[1152]{0:T(1024)} %copy-done.28) | copy-start | bytes 13828
  334.1 55.8 %copy-start.33 = (f32[256]{0:T(256)S(1)}, f32[256]{0:T(256)}, u32[]{:S(2)}) copy-start(f32[256]{0:T(256)} %copy-done.32) | copy-start | bytes 3076
  334.1 55.8 %copy-start.38 = (f32[256]{0:T(256)S(1)}, f32[256]{0:T(256)}, u32[]{:S(2)}) copy-start(f32[256]{0:T(256)} %copy-done.37) | copy-start | bytes 3076
  349.7 20.9 %all-to-all-start.4 = ((bf16[8,256,144]{1,2,0:T(8,128)(2,1)}), bf16[8,256,144]{1,2,0:T(8,128)(2,1)}, u32[]{:S(2)}, u32[]{:S(2)}) async-start(bf16[8,256,144]{1,2,0:T(8,128)(2,1)} %copy.109), calls=%async_computation.4 | async-start | bytes 1179648 | tf_op jit(solution)/shard_map/all_to_all | solution.py:258
  353.9 77.1 %all-gather.15.cloned.1.call-start = ((), (), s32[]{:S(2)}) async-start(), calls=%async_computation.24 | async-start | bytes 2949120 | tf_op jit(solution)/shard_map/all_gather | solution.py:145
  354.6 145.9 %all-gather.7.cloned.1.call-start = ((), (), s32[]{:S(2)}) async-start(), calls=%async_computation.15 | async-start | bytes 2949120 | tf_op jit(solution)/shard_map/all_gather | solution.py:145
  389.9 6.5 copy-start.36
  399.0 170.6 %all-gather.13.cloned.1.call-start = ((), (), s32[]{:S(2)}) async-start(), calls=%async_computation.21 | async-start | bytes 5308416 | tf_op jit(solution)/shard_map/all_gather | solution.py:136
  399.6 232.7 %reduce-scatter.8.cloned.1.call-start = ((), (), s32[]{:S(2)}) async-start(), calls=%async_computation.18 | async-start | bytes 1474560 | tf_op jit(solution)/shard_map/reduce_scatter | solution.py:157
  405.9 15.5 %all-to-all-start.7 = ((bf16[256,4,288]{0,2,1:T(8,128)(2,1)}), bf16[256,4,288]{0,2,1:T(8,128)(2,1)S(1)}, u32[]{:S(2)}, u32[]{:S(2)}) async-start(bf16[256,4,288]{0,2,1:T(8,128)(2,1)} %bitcast.33), calls=%async_computation.9 | async-start | bytes 1179648 | tf_op jit(solution)/shard_map/all_to_all | solution.py:144
  421.3 44.1 %all-to-all-start.9 = ((bf16[256,4,1152]{2,0,1:T(8,128)(2,1)}), bf16[256,4,1152]{2,0,1:T(8,128)(2,1)S(1)}, u32[]{:S(2)}, u32[]{:S(2)}) async-start(bf16[256,4,1152]{2,0,1:T(8,128)(2,1)} %bitcast.164), calls=%async_computation.13 | async-start | bytes 4718592 | tf_op jit(solution)/shard_map/all_to_all | solution.py:144
  425.0 216.3 %reduce-scatter.10.cloned.1.call-start = ((), (), s32[]{:S(2)}) async-start(), calls=%async_computation.20 | async-start | bytes 995328 | tf_op jit(solution)/shard_map/reduce_scatter | solution.py:147
  430.7 225.3 %reduce-scatter.14.cloned.1.call-start = ((), (), s32[]{:S(2)}) async-start(), calls=%async_computation.23 | async-start | bytes 2985984 | tf_op jit(solution)/shard_map/reduce_scatter | solution.py:147
  465.5 6.5 copy-start.26
  474.4 18.1 %all-to-all-start.6 = ((bf16[256,4,576]{0,2,1:T(8,128)(2,1)}), bf16[256,4,576]{0,2,1:T(8,128)(2,1)S(1)}, u32[]{:S(2)}, u32[]{:S(2)}) async-start(bf16[256,4,576]{0,2,1:T(8,128)(2,1)} %pad_maximum_fusion), calls=%async_computation.6 | async-start | bytes 2359296 | tf_op jit(solution)/shard_map/all_to_all | solution.py:144
  493.5 74.3 %all-to-all-start.8 = ((bf16[256,8,576]{0,2,1:T(8,128)(2,1)}), bf16[256,8,576]{0,2,1:T(8,128)(2,1)S(1)}, u32[]{:S(2)}, u32[]{:S(2)}) async-start(bf16[256,8,576]{0,2,1:T(8,128)(2,1)} %bitcast.35), calls=%async_computation.11 | async-start | bytes 4718592 | tf_op jit(solution)/shard_map/all_to_all | solution.py:137
  498.0 183.5 %reduce-scatter.6.cloned.1.call-start = ((), (), s32[]{:S(2)}) async-start(), calls=%async_computation.16 | async-start | bytes 1658880 | tf_op jit(solution)/shard_map/reduce_scatter | solution.py:147
  500.5 5.7 copy-start.44
  505.8 207.2 %reduce-scatter.12.cloned.1.call-start = ((), (), s32[]{:S(2)}) async-start(), calls=%async_computation.22 | async-start | bytes 1843200 | tf_op jit(solution)/shard_map/reduce_scatter | solution.py:139
  569.6 8.3 %copy-start.8 = (f32[256,1152]{1,0:T(8,128)S(1)}, f32[256,1152]{1,0:T(8,128)}, u32[]{:S(2)}) copy-start(f32[256,1152]{1,0:T(8,128)} %copy-done.6) | copy-start | bytes 3538948
  577.9 9.0 %copy-start.30 = (f32[1152]{0:T(1024)S(1)}, f32[1152]{0:T(1024)}, u32[]{:S(2)}) copy-start(f32[1152]{0:T(1024)} %get-tuple-element.281) | copy-start | bytes 13828
  577.9 9.0 %copy-start.40 = (f32[1152]{0:T(1024)S(1)}, f32[1152]{0:T(1024)}, u32[]{:S(2)}) copy-start(f32[1152]{0:T(1024)} %get-tuple-element.235) | copy-start | bytes 13828
  577.9 9.0 %copy-start.39 = (f32[1152]{0:T(1024)S(1)}, f32[1152]{0:T(1024)}, u32[]{:S(2)}) copy-start(f32[1152]{0:T(1024)} %get-tuple-element.239) | copy-start | bytes 13828
  577.9 9.0 %copy-start.31 = (f32[4608]{0:T(1024)S(1)}, f32[4608]{0:T(1024)}, u32[]{:S(2)}) copy-start(f32[4608]{0:T(1024)} %get-tuple-element.318) | copy-start | bytes 55300
  577.9 48.5 %copy-start.22 = (bf16[256,1152]{1,0:T(8,128)(2,1)S(1)}, bf16[256,1152]{1,0:T(8,128)(2,1)}, u32[]{:S(2)}) copy-start(bf16[256,1152]{1,0:T(8,128)(2,1)} %get-tuple-element.284) | copy-start | bytes 1769476
  630.8 84.1 %copy-start.1 = (bf16[1152,1152]{1,0:T(8,128)(2,1)S(1)}, bf16[1152,1152]{1,0:T(8,128)(2,1)}, u32[]{:S(2)}) copy-start(bf16[1152,1152]{1,0:T(8,128)(2,1)} %param.29) | copy-start | bytes 7962628
  634.5 19.3 %collective-permute-start.2 = (f32[288,144]{1,0:T(8,128)}, f32[288,144]{1,0:T(8,128)}, u32[]{:S(2)}, u32[]{:S(2)}) collective-permute-start(f32[288,144]{1,0:T(8,128)} %get-tuple-element.301), channel_id=1, source_target_pairs={{0,8},{4,20},{8,0},{12,12},{16,24},{20,4},{24,16},{28,28},{1,9},{5... | collective-permute-start | bytes 497672 | tf_op jit(solution)/shard_map/ppermute | solution.py:168
  639.2 14.6 %collective-permute-start.1 = (f32[288,144]{1,0:T(8,128)S(1)}, f32[288,144]{1,0:T(8,128)}, u32[]{:S(2)}, u32[]{:S(2)}) collective-permute-start(f32[288,144]{1,0:T(8,128)S(1)} %get-tuple-element.302), channel_id=1, source_target_pairs={{0,20},{4,0},{8,12},{12,24},{16,4},{20,16},{24,28},{28,8},{1,21},{... | collective-permute-start | bytes 497672 | tf_op jit(solution)/shard_map/ppermute | solution.py:168
  639.3 14.5 %collective-permute-start = (f32[288,144]{1,0:T(8,128)S(1)}, f32[288,144]{1,0:T(8,128)}, u32[]{:S(2)}, u32[]{:S(2)}) collective-permute-start(f32[288,144]{1,0:T(8,128)S(1)} %get-tuple-element.300), channel_id=1, source_target_pairs={{0,0},{4,12},{8,24},{12,4},{16,16},{20,28},{24,8},{28,20},{1,1},{5... | collective-permute-start | bytes 497672 | tf_op jit(solution)/shard_map/ppermute | solution.py:168
  (38 other events, 110.3 us)
Sparse Core Ops, SparseCore 0:
  143.6 53.6 all-gather.8
  222.6 38.7 all-gather.10
  356.5 38.7 all-gather.14
  399.2 66.5 all-gather.6
  467.8 65.8 all-gather.12
  536.5 34.6 reduce-scatter.7
  573.5 32.1 reduce-scatter.9
  608.0 37.3 reduce-scatter.13
  647.7 33.7 reduce-scatter.5
  684.3 28.6 reduce-scatter.11
where the time goes:
time: 729 us; the launch traced here: 722 us
  waiting for transfers between devices  290 us (40%)
  matrix products  195 us (27%)
  local copies, waits for them, and re-layouts  64.7 us (9%)
  blocking collectives  58.1 us (8%)
  other arithmetic  52 us (7%)
  starting transfers between devices  46.1 us (6%)
  between operations  15.3 us (2%)
    all_to_all x1, waiting for transfers between devices, seq_gathered_grad(): lax.all_to_all(right, 'seq', split_axis=1, concat_axis=0, tiled=True)  61.5 us
    all_to_all x3, waiting for transfers between devices, batch_gathered_grad(): lax.all_to_all(left, 'batch', split_axis=1, concat_axis=0, tiled=True)  54.5 us
    all_to_all x1, waiting for transfers between devices, on_device(): lax.all_to_all(packed.reshape(local_rows, 3, seq_count, feature_count //...  41.7 us
    dot_general x5, matrix products, product(): return jnp.dot(left, right, preferred_element_type=jnp.float32)  40.6 us
    psum x1, blocking collectives, on_device(): small_total = lax.psum(jnp.concatenate(small_grads), ('seq', 'batch'))  38.9 us
    dot_general x5, matrix products, times_transposed(): lax.dot_general(left, right, (((1,), (1,)), ((), ())), preferred_element_...  37.2 us
    dot_general x5, matrix products, contract_rows(): lax.dot_general(left, right, (((0,), (0,)), ((), ())), preferred_element_...  30.8 us
    reduce_scatter x1, waiting for transfers between devices, seq_gathered_grad(): summed = lax.psum_scatter(partial, 'batch', scatter_dimension=0, tiled=True)  29.8 us
  transfers between devices with their start and end apart: 22, of which 12 were waited for; matrix products, arithmetic and copies ran while one was open for 31% of the time, Pallas kernels for 0%

commit v1 on v0

--- a/solution.py
+++ b/solution.py
@@ -3,6 +3,7 @@
 import jax.numpy as jnp
 from jax import lax
 from jax.sharding import PartitionSpec as P
+from jax.lax import all_gather
 
 HD = 72
 norm_eps = 1e-05
@@ -289,7 +290,9 @@
         grad_down_bias,
     )
     small_sizes = [piece.shape[0] for piece in small_grads]
-    small_total = lax.psum(jnp.concatenate(small_grads), ("seq", "batch"))
+    small_total = jnp.sum(
+        all_gather(jnp.concatenate(small_grads), axis_name=("seq", "batch")), axis=0
+    )
     summed_small = []
     offset = 0
     for size in small_sizes:

time: 729 us -> 783 us (1.074)
  waiting for transfers between devices: 290 us -> 370 us
  blocking collectives: 58.1 us -> 37.1 us
    psum x1 -> x0, blocking collectives: 38.9 us -> none  [on_device(): small_total = lax.psum(jnp.concatenate(small_grads), ('seq', 'batch'))]
    all_gather x0 -> x1, waiting for transfers between devices: none -> 31.8 us  [on_device(): all_gather(jnp.concatenate(small_grads), axis_name=('seq', 'batch'))]
    reduce_scatter x3, waiting for transfers between devices: 23.6 us -> 52.2 us  [batch_gathered_grad(): summed = lax.psum_scatter(partial, 'seq', scatter_dimension=1, tiled=True)]
    reduce_scatter x1, waiting for transfers between devices: 0.01 us -> 27.5 us  [qkv_grad_from_heads(): summed = lax.psum_scatter(partial, 'batch', scatter_dimension=0, tiled=True)]
    all_to_all x3 -> x2, waiting for transfers between devices: 54.5 us -> 35.7 us  [batch_gathered_grad(): lax.all_to_all(left, 'batch', split_axis=1, concat_axis=0, tiled=True)]
    all_to_all x0 -> x1, blocking collectives: none -> 17.9 us  [batch_gathered_grad(): lax.all_to_all(left, 'batch', split_axis=1, concat_axis=0, tiled=True)]
    ppermute x3, waiting for transfers between devices: 10.9 us -> 21.3 us  [qkv_grad_from_heads(): slots.append(lax.ppermute(sent, 'seq', pairs))]
  transfers between devices with their start and end apart: 22 -> 22, of which waited for: 12 -> 15; matrix products, arithmetic and copies ran while one was open for 31% -> 23% of each run, Pallas kernels for 0% -> 0%
where the time goes in v1:
time: 783 us; the launch traced here: 777 us
  waiting for transfers between devices  370 us (47%)
  matrix products  194 us (25%)
  local copies, waits for them, and re-layouts  64.7 us (8%)
  other arithmetic  52.7 us (7%)
  starting transfers between devices  41.9 us (5%)
  blocking collectives  37.1 us (5%)
  between operations  15 us (2%)
    all_to_all x1, waiting for transfers between devices, seq_gathered_grad(): lax.all_to_all(right, 'seq', split_axis=1, concat_axis=0, tiled=True)  66.9 us
    reduce_scatter x3, waiting for transfers between devices, batch_gathered_grad(): summed = lax.psum_scatter(partial, 'seq', scatter_dimension=1, tiled=True)  52.2 us
    all_to_all x1, waiting for transfers between devices, on_device(): lax.all_to_all(packed.reshape(local_rows, 3, seq_count, feature_count //...  41.7 us
    dot_general x5, matrix products, product(): return jnp.dot(left, right, preferred_element_type=jnp.float32)  40.6 us
    dot_general x5, matrix products, times_transposed(): lax.dot_general(left, right, (((1,), (1,)), ((), ())), preferred_element_...  35.8 us
    all_to_all x2, waiting for transfers between devices, batch_gathered_grad(): lax.all_to_all(left, 'batch', split_axis=1, concat_axis=0, tiled=True)  35.7 us
    all_gather x1, waiting for transfers between devices, on_device(): all_gather(jnp.concatenate(small_grads), axis_name=('seq', 'batch'))  31.8 us
    dot_general x5, matrix products, contract_rows(): lax.dot_general(left, right, (((0,), (0,)), ((), ())), preferred_element_...  31.2 us
  transfers between devices with their start and end apart: 22, of which 15 were waited for; matrix products, arithmetic and copies ran while one was open for 23% of the time, Pallas kernels for 0%

profile of v1, /device:TPU:0, one launch (start us, length us, event | category | flops | bytes accessed | tf_op | source)
XLA Modules:
  0.0 776.6 jit_solution(15446802588496685752)
XLA Ops:
  9.4 4.7 fusion.79
  16.0 7.3 convolution_convert_fusion.1
  30.0 6.6 all-to-all-start
  36.9 41.7 %all-to-all-done = bf16[256,3,8,144]{0,3,1,2:T(8,128)(2,1)} async-done(((bf16[256,3,8,144]{0,3,1,2:T(8,128)(2,1)}), bf16[256,3,8,144]{0,3,1,2:T(8,128)(2,1)}, u32[]{:S(2)}, u32[]{:S(2)}) %all-to-all-start) | async-done | bytes 1769504 | tf_op jit(solution)/shard_map/all_to_all | solution.py:212
  93.9 36.5 %while.27 = (s32[]{:T(128)}, bf16[4,512,144]{1,2,0:T(8,128)(2,1)}, f32[4,2,512,1]{2,1,3,0:T(2,128)S(1)}, s32[4,512]{1,0:T(4,128)S(1)}, s32[2048]{0:T(1024)S(1)},...) while((s32[]{:T(128)}, bf16[4,512,144]{1,2,0:T(8,128)(2,1)}, ...), condition=%wide.region_7.8_spmd, body=%wide.region_4.7_spmd.sunk | while | flops 628169728 | bytes 33536144 | solution.py:75
  137.1 4.2 all-to-all-start.1
  141.6 16.4 %all-to-all-done.1 = bf16[8,256,144]{1,2,0:T(8,128)(2,1)} async-done(((bf16[8,256,144]{1,2,0:T(8,128)(2,1)}), bf16[8,256,144]{1,2,0:T(8,128)(2,1)}, u32[]{:S(2)}, u32[]{:S(2)}) %all-to-all-start.1) | async-done | bytes 589856 | tf_op jit(solution)/shard_map/all_to_all | solution.py:224
  162.7 17.2 %multiply_convert_fusion.1 = (bf16[256,4608]{1,0:T(8,128)(2,1)}, f32[256,4608]{1,0:T(8,128)}, f32[256,4608]{1,0:T(8,128)}) fusion(f32[4608]{0:T(1024)S(1)} %convert_element_type.134, bf16[256,1152]{1,0:T(8,128)(2,1)} %add_convert_fusion.2, bf16[1152,4608]{1,0:T(8,128)(2,1)} %param.33), kind=kOutput, calls=%fused_computation.57 | convolution fusion | flops 2795765760 | bytes 23021568 | tf_op jit(solution)/shard_map/dot_general | solution.py:13
  179.9 14.0 %convert_reduce_fusion = (f32[4608]{0:T(1024)S(1)}, bf16[256,4608]{1,0:T(8,128)(2,1)}) fusion(f32[256,4608]{1,0:T(8,128)} %get-tuple-element.290, f32[256,4608]{1,0:T(8,128)} %get-tuple-element.315, bf16[4608,1152]{1,0:T(8,128)(2,1)} %param.35, bf16[1,256,1152]{2,1,0:T(8,128)(2,1)S(1)} %copy-done.14), kind=kOutput, calls=%fused_computation.55 | convolution fusion | flops 2736778752 | bytes 23021568 | tf_op jit(solution)/shard_map/dot_general | solution.py:23
  193.9 8.1 %multiply_reduce_fusion.1 = (f32[1152]{0:T(1024)S(1)}, f32[256]{0:T(256)S(1)}, f32[1152]{0:T(1024)S(1)}, f32[256,1152]{1,0:T(8,128)S(1)}) fusion(f32[256,1152]{1,0:T(8,128)S(1)} %copy-done.7, f32[256]{0:T(256)S(1)} %fusion.69, f32[256]{0:T(256)S(1)} %broadcast_multiply_fusion, f32[1152]{0:T(1024)S(1)} %convert_element_type.131, ...), kind=kOutput, calls=%fused_computation.106 | convolution fusion | flops 2720265728 | bytes 15352320 | tf_op jit(solution)/shard_map/dot_general | solution.py:23
  214.0 15.9 %all-to-all-done.2 = bf16[256,8,144]{0,2,1:T(8,128)(2,1)S(1)} async-done(((bf16[256,8,144]{0,2,1:T(8,128)(2,1)}), bf16[256,8,144]{0,2,1:T(8,128)(2,1)S(1)}, u32[]{:S(2)}, u32[]{:S(2)}) %all-to-all-start.2) | async-done | bytes 589856 | tf_op jit(solution)/shard_map/all_to_all | solution.py:250
  232.2 87.6 %while.28 = (s32[]{:T(128)}, f32[2048,2,72]{0,2,1:T(8,128)S(1)}, f32[2048,2,72]{0,2,1:T(8,128)}, bf16[4,512,144]{1,2,0:T(8,128)(2,1)}, bf16[4,512,2,72]{1,3,2,0:...) while((s32[]{:T(128)}, f32[2048,2,72]{0,2,1:T(8,128)S(1)}, ...), condition=%wide.region_14.15_spmd.clone, body=%wide.region_12.14_spmd.clone.sunk | while | flops 1543781376 | bytes 136800560 | solution.py:121
  235.2 4.3 multiply_reduce_fusion.8
  239.5 3.9 multiply_convert_fusion.4
  246.8 5.4 fusion.146
  257.3 4.3 multiply_reduce_fusion.8
  268.9 5.2 fusion.146
  279.2 4.3 multiply_reduce_fusion.8
  290.8 5.2 fusion.146
  301.0 4.3 multiply_reduce_fusion.8
  312.6 5.2 fusion.146
  322.3 4.3 all-to-all-start.5
  327.9 15.5 %all-to-all-done.5 = bf16[8,256,144]{1,2,0:T(8,128)(2,1)} async-done(((bf16[8,256,144]{1,2,0:T(8,128)(2,1)}), bf16[8,256,144]{1,2,0:T(8,128)(2,1)}, u32[]{:S(2)}, u32[]{:S(2)}) %all-to-all-start.5) | async-done | bytes 589856 | tf_op jit(solution)/shard_map/all_to_all | solution.py:260
  343.4 4.2 all-to-all-start.4
  351.0 13.3 %all-to-all-done.4 = bf16[8,256,144]{1,2,0:T(8,128)(2,1)} async-done(((bf16[8,256,144]{1,2,0:T(8,128)(2,1)}), bf16[8,256,144]{1,2,0:T(8,128)(2,1)}, u32[]{:S(2)}, u32[]{:S(2)}) %all-to-all-start.4) | async-done | bytes 589856 | tf_op jit(solution)/shard_map/all_to_all | solution.py:259
  364.3 19.3 %all_to_all.180 = bf16[8,256,144]{1,2,0:T(8,128)(2,1)S(1)} all-to-all(bf16[8,256,144]{1,2,0:T(8,128)(2,1)S(1)} %copy.108), channel_id=1, replica_groups=mesh['seq'=8,'batch'=4] {'seq'}, dimensions={0} | all-to-all | bytes 1179648 | tf_op jit(solution)/shard_map/all_to_all | solution.py:258
  383.6 6.5 multiply_reduce_fusion.2
  393.4 17.9 %all_to_all.181 = bf16[256,4,288]{0,2,1:T(8,128)(2,1)S(1)} all-to-all(bf16[256,4,288]{0,2,1:T(8,128)(2,1)} %bitcast.33), channel_id=1, replica_groups=mesh['seq'=8,'batch'=4] {'batch'}, dimensions={1} | all-to-all | bytes 1179648 | tf_op jit(solution)/shard_map/all_to_all | solution.py:145
  412.1 4.4 convolution_convert_fusion.5
  419.0 4.7 all-to-all-start.9
  423.9 6.1 convolution_convert_fusion.4
  430.3 25.6 %all-to-all-done.9 = bf16[256,4,1152]{2,0,1:T(8,128)(2,1)} async-done(((bf16[256,4,1152]{2,0,1:T(8,128)(2,1)}), bf16[256,4,1152]{2,0,1:T(8,128)(2,1)}, u32[]{:S(2)}, u32[]{:S(2)}) %all-to-all-start.9) | async-done | bytes 2359328 | tf_op jit(solution)/shard_map/all_to_all | solution.py:145
  455.9 7.2 convolution_convert_fusion
  469.1 4.3 copy.116
  473.4 10.1 %all-to-all-done.6 = bf16[256,4,576]{0,2,1:T(8,128)(2,1)S(1)} async-done(((bf16[256,4,576]{0,2,1:T(8,128)(2,1)}), bf16[256,4,576]{0,2,1:T(8,128)(2,1)S(1)}, u32[]{:S(2)}, u32[]{:S(2)}) %all-to-all-start.6) | async-done | bytes 1179680 | tf_op jit(solution)/shard_map/all_to_all | solution.py:145
  484.5 4.7 all-to-all-start.8
  491.8 5.3 convolution_convert_fusion.3
  497.4 66.9 %all-to-all-done.8 = bf16[256,8,576]{0,2,1:T(8,128)(2,1)S(1)} async-done(((bf16[256,8,576]{0,2,1:T(8,128)(2,1)}), bf16[256,8,576]{0,2,1:T(8,128)(2,1)S(1)}, u32[]{:S(2)}, u32[]{:S(2)}) %all-to-all-start.8) | async-done | bytes 2359328 | tf_op jit(solution)/shard_map/all_to_all | solution.py:138
  565.9 8.2 %convolution_convert_fusion.2 = bf16[1152,576]{1,0:T(8,128)(2,1)} fusion(bf16[2048,1152]{1,0:T(8,128)(2,1)} %all-gather.16.cloned.1.call-done, bf16[2048,576]{0,1:T(8,128)(2,1)} %bitcast.218), kind=kOutput, calls=%fused_computation.71 | convolution fusion | flops 2718572544 | bytes 8404992 | tf_op jit(solution)/shard_map/dot_general | solution.py:17
  574.3 8.9 %fusion.47 = bf16[1,256,1152]{2,1,0:T(8,128)(2,1)} fusion(f32[256,1152]{1,0:T(8,128)S(1)} %copy-done.8, bf16[256,4608]{1,0:T(8,128)(2,1)} %get-tuple-element.289, bf16[4608,1152]{1,0:T(8,128)(2,1)} %param.35, f32[1152]{0:T(1024)S(1)} %convert_element_type.136), kind=kOutput, calls=%fused_computation.82 | convolution fusion | flops 2718793728 | bytes 14750208 | tf_op jit(solution)/shard_map/dot_general | solution.py:13
  583.2 4.3 fusion.81
  590.6 31.8 %all-gather.20.cloned.1.call-done = f32[32,1,12672]{2,1,0:T(1,128)} async-done(((f32[1,1,12672]{2,1,0:T(1,128)}), f32[32,1,12672]{2,1,0:T(1,128)}) %all-gather.20.cloned.1.call-update) | async-done | bytes 1622032 | tf_op jit(solution)/shard_map/all_gather | solution.py:294
  625.6 27.5 %reduce-scatter.8.cloned.1.call-done = bf16[288,432]{1,0:T(8,128)(2,1)} async-done(((bf16[1152,432]{1,0:T(8,128)(2,1)}), bf16[288,432]{1,0:T(8,128)(2,1)}) %reduce-scatter.8.cloned.1.call-update) | async-done | bytes 248848 | tf_op jit(solution)/shard_map/reduce_scatter | solution.py:158
  659.6 16.3 %collective-permute-done.2 = f32[288,144]{1,0:T(8,128)S(1)} collective-permute-done((f32[288,144]{1,0:T(8,128)S(1)}, f32[288,144]{1,0:T(8,128)S(1)}, u32[]{:S(2)}, u32[]{:S(2)}) %collective-permute-start.2) | collective-permute-done | bytes 165920 | tf_op jit(solution)/shard_map/ppermute | solution.py:169
  675.9 5.0 collective-permute-done.1
  682.0 18.9 %reduce-scatter.14.cloned.1.call-done = bf16[1152,144]{0,1:T(8,128)(2,1)} async-done(((bf16[1152,1152]{0,1:T(8,128)(2,1)}), bf16[1152,144]{0,1:T(8,128)(2,1)}) %reduce-scatter.14.cloned.1.call-update) | async-done | bytes 331792 | tf_op jit(solution)/shard_map/reduce_scatter | solution.py:148
  702.8 33.3 %reduce-scatter.6.cloned.1.call-done = bf16[576,144]{0,1:T(8,128)(2,1)} async-done(((bf16[576,1152]{0,1:T(8,128)(2,1)}), bf16[576,144]{0,1:T(8,128)(2,1)}) %reduce-scatter.6.cloned.1.call-update) | async-done | bytes 165904 | tf_op jit(solution)/shard_map/reduce_scatter | solution.py:148
  737.8 30.2 %reduce-scatter.12.cloned.1.call-done = bf16[288,576]{1,0:T(8,128)(2,1)} async-done(((bf16[1152,576]{1,0:T(8,128)(2,1)}), bf16[288,576]{1,0:T(8,128)(2,1)}) %reduce-scatter.12.cloned.1.call-update) | async-done | bytes 331792 | tf_op jit(solution)/shard_map/reduce_scatter | solution.py:140
  (299 shorter events, 178.6 us)
Async XLA Ops:
  7.2 150.8 %copy-start = (bf16[1152,1152]{1,0:T(8,128)(2,1)S(1)}, bf16[1152,1152]{1,0:T(8,128)(2,1)}, u32[]{:S(2)}) copy-start(bf16[1152,1152]{1,0:T(8,128)(2,1)} %param.29) | copy-start | bytes 7962628
  9.4 5.6 copy-start.28
  16.0 7.3 copy-start.22
  27.1 9.5 %copy-start.41 = (s32[1,4]{1,0:T(1,128)S(1)}, s32[1,4]{1,0:T(1,128)}, u32[]{:S(2)}) copy-start(s32[1,4]{1,0:T(1,128)} %param.23) | copy-start | bytes 52
  30.0 48.6 %all-to-all-start = ((bf16[256,3,8,144]{0,3,1,2:T(8,128)(2,1)}), bf16[256,3,8,144]{0,3,1,2:T(8,128)(2,1)}, u32[]{:S(2)}, u32[]{:S(2)}) async-start(bf16[256,3,8,144]{0,3,1,2:T(8,128)(2,1)} %copy.98), calls=%async_computation | async-start | bytes 3538944 | tf_op jit(solution)/shard_map/all_to_all | solution.py:212
  130.5 11.1 %copy-start.37 = (bf16[1152]{0:T(1024)(128)(2,1)S(1)}, bf16[1152]{0:T(1024)(128)(2,1)}, u32[]{:S(2)}) copy-start(bf16[1152]{0:T(1024)(128)(2,1)} %param.30) | copy-start | bytes 6916
  130.5 11.1 %copy-start.32 = (bf16[4608]{0:T(1024)(128)(2,1)S(1)}, bf16[4608]{0:T(1024)(128)(2,1)}, u32[]{:S(2)}) copy-start(bf16[4608]{0:T(1024)(128)(2,1)} %param.34) | copy-start | bytes 27652
  130.5 11.1 %copy-start.38 = (bf16[1152]{0:T(1024)(128)(2,1)S(1)}, bf16[1152]{0:T(1024)(128)(2,1)}, u32[]{:S(2)}) copy-start(bf16[1152]{0:T(1024)(128)(2,1)} %param.32) | copy-start | bytes 6916
  130.5 11.1 %copy-start.39 = (bf16[1152]{0:T(1024)(128)(2,1)S(1)}, bf16[1152]{0:T(1024)(128)(2,1)}, u32[]{:S(2)}) copy-start(bf16[1152]{0:T(1024)(128)(2,1)} %param.31) | copy-start | bytes 6916
  137.1 20.9 %all-to-all-start.1 = ((bf16[8,256,144]{1,2,0:T(8,128)(2,1)}), bf16[8,256,144]{1,2,0:T(8,128)(2,1)}, u32[]{:S(2)}, u32[]{:S(2)}) async-start(bf16[8,256,144]{1,2,0:T(8,128)(2,1)} %copy.102), calls=%async_computation.1 | async-start | bytes 1179648 | tf_op jit(solution)/shard_map/all_to_all | solution.py:224
  141.3 270.9 %all-gather.14.cloned.1.call-start = ((), (), s32[]{:S(2)}) async-start(), calls=%async_computation.19 | async-start | bytes 2949120 | tf_op jit(solution)/shard_map/all_gather | solution.py:146
  162.7 17.2 %copy-start.14 = (bf16[1,256,1152]{2,1,0:T(8,128)(2,1)S(1)}, bf16[1,256,1152]{2,1,0:T(8,128)(2,1)}, u32[]{:S(2)}) copy-start(bf16[1,256,1152]{2,1,0:T(8,128)(2,1)} %param.37) | copy-start | bytes 1769476
  179.9 14.0 %copy-start.7 = (f32[256,1152]{1,0:T(8,128)S(1)}, f32[256,1152]{1,0:T(8,128)}, u32[]{:S(2)}) copy-start(f32[256,1152]{1,0:T(8,128)} %copy-done.6) | copy-start | bytes 3538948
  209.6 20.2 %all-to-all-start.2 = ((bf16[256,8,144]{0,2,1:T(8,128)(2,1)}), bf16[256,8,144]{0,2,1:T(8,128)(2,1)S(1)}, u32[]{:S(2)}, u32[]{:S(2)}) async-start(bf16[256,8,144]{0,2,1:T(8,128)(2,1)} %bitcast.18), calls=%async_computation.2 | async-start | bytes 1179648 | tf_op jit(solution)/shard_map/all_to_all | solution.py:250
  213.2 210.6 %all-gather.12.cloned.1.call-start = ((), (), s32[]{:S(2)}) async-start(), calls=%async_computation.17 | async-start | bytes 5308416 | tf_op jit(solution)/shard_map/all_gather | solution.py:156
  246.8 5.5 copy-start.3
  268.9 5.2 copy-start.3
  321.2 6.6 copy-start.17
  322.3 26.1 %copy-start.13 = (bf16[4,512,144]{1,2,0:T(8,128)(2,1)S(1)}, bf16[4,512,144]{1,2,0:T(8,128)(2,1)}, u32[]{:S(2)}) copy-start(bf16[4,512,144]{1,2,0:T(8,128)(2,1)} %get-tuple-element.120) | copy-start | bytes 1769476
  322.3 21.1 %all-to-all-start.5 = ((bf16[8,256,144]{1,2,0:T(8,128)(2,1)}), bf16[8,256,144]{1,2,0:T(8,128)(2,1)}, u32[]{:S(2)}, u32[]{:S(2)}) async-start(bf16[8,256,144]{1,2,0:T(8,128)(2,1)} %copy.110), calls=%async_computation.5 | async-start | bytes 1179648 | tf_op jit(solution)/shard_map/all_to_all | solution.py:260
  326.8 24.2 %copy-start.19 = (bf16[2048,2,72]{0,2,1:T(8,128)(2,1)}, bf16[2048,2,72]{0,2,1:T(8,128)(2,1)S(1)}, u32[]{:S(2)}) copy-start(bf16[2048,2,72]{0,2,1:T(8,128)(2,1)S(1)} %multiply_convert_fusion.2) | copy-start | bytes 1769476
  327.8 55.8 %copy-start.10 = (f32[256,1152]{1,0:T(8,128)S(1)}, f32[256,1152]{1,0:T(8,128)}, u32[]{:S(2)}) copy-start(f32[256,1152]{1,0:T(8,128)} %copy-done.9) | copy-start | bytes 3538948
  327.8 55.8 %copy-start.29 = (f32[1152]{0:T(1024)S(1)}, f32[1152]{0:T(1024)}, u32[]{:S(2)}) copy-start(f32[1152]{0:T(1024)} %copy-done.28) | copy-start | bytes 13828
  327.8 55.8 %copy-start.31 = (f32[256]{0:T(256)S(1)}, f32[256]{0:T(256)}, u32[]{:S(2)}) copy-start(f32[256]{0:T(256)} %copy-done.30) | copy-start | bytes 3076
  327.8 55.8 %copy-start.36 = (f32[256]{0:T(256)S(1)}, f32[256]{0:T(256)}, u32[]{:S(2)}) copy-start(f32[256]{0:T(256)} %copy-done.35) | copy-start | bytes 3076
  343.4 20.9 %all-to-all-start.4 = ((bf16[8,256,144]{1,2,0:T(8,128)(2,1)}), bf16[8,256,144]{1,2,0:T(8,128)(2,1)}, u32[]{:S(2)}, u32[]{:S(2)}) async-start(bf16[8,256,144]{1,2,0:T(8,128)(2,1)} %copy.109), calls=%async_computation.4 | async-start | bytes 1179648 | tf_op jit(solution)/shard_map/all_to_all | solution.py:259
  347.6 82.7 %all-gather.18.cloned.1.call-start = ((), (), s32[]{:S(2)}) async-start(), calls=%async_computation.24 | async-start | bytes 2949120 | tf_op jit(solution)/shard_map/all_gather | solution.py:146
  348.3 143.4 %all-gather.10.cloned.1.call-start = ((), (), s32[]{:S(2)}) async-start(), calls=%async_computation.15 | async-start | bytes 2949120 | tf_op jit(solution)/shard_map/all_gather | solution.py:146
  383.6 6.5 copy-start.34
  392.7 173.2 %all-gather.16.cloned.1.call-start = ((), (), s32[]{:S(2)}) async-start(), calls=%async_computation.21 | async-start | bytes 5308416 | tf_op jit(solution)/shard_map/all_gather | solution.py:137
  393.3 195.7 %reduce-scatter.10.cloned.1.call-start = ((), (), s32[]{:S(2)}) async-start(), calls=%async_computation.20 | async-start | bytes 995328 | tf_op jit(solution)/shard_map/reduce_scatter | solution.py:148
  412.1 5.3 copy-start.21
  416.5 205.9 %all-gather.20.cloned.1.call-start = ((), (), s32[]{:S(2)}) async-start(), calls=%async_computation.25 | async-start | bytes 1672704 | tf_op jit(solution)/shard_map/all_gather | solution.py:294
  419.0 36.9 %all-to-all-start.9 = ((bf16[256,4,1152]{2,0,1:T(8,128)(2,1)}), bf16[256,4,1152]{2,0,1:T(8,128)(2,1)}, u32[]{:S(2)}, u32[]{:S(2)}) async-start(bf16[256,4,1152]{2,0,1:T(8,128)(2,1)} %bitcast.164), calls=%async_computation.13 | async-start | bytes 4718592 | tf_op jit(solution)/shard_map/all_to_all | solution.py:145
  423.7 229.4 %reduce-scatter.8.cloned.1.call-start = ((), (), s32[]{:S(2)}) async-start(), calls=%async_computation.18 | async-start | bytes 1474560 | tf_op jit(solution)/shard_map/reduce_scatter | solution.py:158
  430.0 270.9 %reduce-scatter.14.cloned.1.call-start = ((), (), s32[]{:S(2)}) async-start(), calls=%async_computation.23 | async-start | bytes 2985984 | tf_op jit(solution)/shard_map/reduce_scatter | solution.py:148
  455.9 7.3 copy-start.26
  465.6 17.9 %all-to-all-start.6 = ((bf16[256,4,576]{0,2,1:T(8,128)(2,1)}), bf16[256,4,576]{0,2,1:T(8,128)(2,1)S(1)}, u32[]{:S(2)}, u32[]{:S(2)}) async-start(bf16[256,4,576]{0,2,1:T(8,128)(2,1)} %pad_maximum_fusion), calls=%async_computation.6 | async-start | bytes 2359296 | tf_op jit(solution)/shard_map/all_to_all | solution.py:145
  484.5 79.7 %all-to-all-start.8 = ((bf16[256,8,576]{0,2,1:T(8,128)(2,1)}), bf16[256,8,576]{0,2,1:T(8,128)(2,1)S(1)}, u32[]{:S(2)}, u32[]{:S(2)}) async-start(bf16[256,8,576]{0,2,1:T(8,128)(2,1)} %bitcast.35), calls=%async_computation.11 | async-start | bytes 4718592 | tf_op jit(solution)/shard_map/all_to_all | solution.py:138
  489.3 246.8 %reduce-scatter.6.cloned.1.call-start = ((), (), s32[]{:S(2)}) async-start(), calls=%async_computation.16 | async-start | bytes 1658880 | tf_op jit(solution)/shard_map/reduce_scatter | solution.py:148
  497.1 270.8 %reduce-scatter.12.cloned.1.call-start = ((), (), s32[]{:S(2)}) async-start(), calls=%async_computation.22 | async-start | bytes 1843200 | tf_op jit(solution)/shard_map/reduce_scatter | solution.py:140
  565.9 8.3 %copy-start.40 = (bf16[1152]{0:T(1024)(128)(2,1)S(1)}, bf16[1152]{0:T(1024)(128)(2,1)}, u32[]{:S(2)}) copy-start(bf16[1152]{0:T(1024)(128)(2,1)} %param.36) | copy-start | bytes 6916
  565.9 8.4 %copy-start.8 = (f32[256,1152]{1,0:T(8,128)S(1)}, f32[256,1152]{1,0:T(8,128)}, u32[]{:S(2)}) copy-start(f32[256,1152]{1,0:T(8,128)} %copy-done.6) | copy-start | bytes 3538948
  574.3 8.9 %copy-start.23 = (bf16[256,1152]{1,0:T(8,128)(2,1)S(1)}, bf16[256,1152]{1,0:T(8,128)(2,1)}, u32[]{:S(2)}) copy-start(bf16[256,1152]{1,0:T(8,128)(2,1)} %get-tuple-element.284) | copy-start | bytes 1769476
  622.5 147.4 %copy-start.1 = (bf16[1152,1152]{1,0:T(8,128)(2,1)S(1)}, bf16[1152,1152]{1,0:T(8,128)(2,1)}, u32[]{:S(2)}) copy-start(bf16[1152,1152]{1,0:T(8,128)(2,1)} %param.29) | copy-start | bytes 7962628
  654.4 21.5 %collective-permute-start.2 = (f32[288,144]{1,0:T(8,128)S(1)}, f32[288,144]{1,0:T(8,128)S(1)}, u32[]{:S(2)}, u32[]{:S(2)}) collective-permute-start(f32[288,144]{1,0:T(8,128)S(1)} %get-tuple-element.301), channel_id=1, source_target_pairs={{0,8},{4,20},{8,0},{12,12},{16,24},{20,4},{24,16},{28,28},{1,9},{5... | collective-permute-start | bytes 497672 | tf_op jit(solution)/shard_map/ppermute | solution.py:169
  657.8 23.1 %collective-permute-start.1 = (f32[288,144]{1,0:T(8,128)S(1)}, f32[288,144]{1,0:T(8,128)S(1)}, u32[]{:S(2)}, u32[]{:S(2)}) collective-permute-start(f32[288,144]{1,0:T(8,128)S(1)} %get-tuple-element.302), channel_id=1, source_target_pairs={{0,20},{4,0},{8,12},{12,24},{16,4},{20,16},{24,28},{28,8},{1,21},{... | collective-permute-start | bytes 497672 | tf_op jit(solution)/shard_map/ppermute | solution.py:169
  658.3 22.6 %collective-permute-start = (f32[288,144]{1,0:T(8,128)S(1)}, f32[288,144]{1,0:T(8,128)S(1)}, u32[]{:S(2)}, u32[]{:S(2)}) collective-permute-start(f32[288,144]{1,0:T(8,128)S(1)} %get-tuple-element.300), channel_id=1, source_target_pairs={{0,0},{4,12},{8,24},{12,4},{16,16},{20,28},{24,8},{28,20},{1,1},{5... | collective-permute-start | bytes 497672 | tf_op jit(solution)/shard_map/ppermute | solution.py:169
  (34 other events, 94.3 us)
Sparse Core Ops, SparseCore 0:
  204.7 36.2 all-gather.13
  242.6 51.1 all-gather.11
  350.2 38.5 all-gather.17
  392.9 57.7 all-gather.9
  452.7 65.3 all-gather.15
  520.2 42.9 reduce-scatter.9
  566.6 55.7 all-gather.19
  625.4 27.6 reduce-scatter.7
  655.4 45.4 reduce-scatter.13
  703.1 32.9 reduce-scatter.5
  739.0 28.8 reduce-scatter.11
